TPU v7x, 128 devices: a whole 4x4x4 slice. The times are simulated.
128 devices in a mesh: node: 32 (over z, y, core), local: 4 (over x).
Axes of the slice: x: 4, y: 4, z: 4, core: 2. Of those that a mesh axis runs over, the one named last changes fastest.
Arguments:
- tokens: bfloat16 [16384, 4096], P(('node', 'local')), may hold values from -6 to 6
- expert_ids: int32 [16384, 8], P(('node', 'local')), may hold values from 0 to 127, all different within a row; in each aligned block of 128 rows (0 to 127, 128 to 255, ...) at most 10 rows name the same one
- gate_scores: float32 [16384, 8], P(('node', 'local')), may hold values from 0.03 to 0.4
- w_gate: bfloat16 [128, 4096, 768], P(('node', 'local')), may hold values from -0.09375 to 0.09375
- w_up: bfloat16 [128, 4096, 768], P(('node', 'local')), may hold values from -0.09375 to 0.09375
- w_down: bfloat16 [128, 768, 4096], P(('node', 'local')), may hold values from -0.21875 to 0.21875
Outputs:
- mixed: bfloat16 [16384, 4096], P(('node', 'local'))
Inputs may be any that keep to these rules, and one draw needn't show every extreme that they name: `expert_ids`: each row names 8 different experts. Among the 128 rows of one device no expert is named more than 10 times, and that many is reached on some device.
All inputs are finite; a program needn't handle non-finite values.
Results may differ from a plain program's by a relative error of at most 0.0058.
Values may be sent and summed in bfloat16 or wider, within the bound.
A program may use at most 128 MiB of HBM per device.

v0:
```python
import jax
import jax.numpy as jnp
from jax import lax
from jax.sharding import PartitionSpec as P


def per_device(tokens, expert_ids, gate_scores, w_gate, w_up, w_down):
    node_count = lax.axis_size("node")
    local_count = lax.axis_size("local")
    experts = node_count * local_count
    token_count = tokens.shape[0]
    features = tokens.shape[1]
    top_count = expert_ids.shape[1]
    capacity = 5 * token_count * top_count // (4 * experts)
    flat_ids = expert_ids.reshape(-1)
    onehot = (flat_ids[:, None] == jnp.arange(experts, dtype=jnp.int32)[None, :]).astype(jnp.int32)
    before = jnp.cumsum(onehot, axis=0) - onehot
    slot_rank = jnp.sum(before * onehot, axis=1)
    slot_index = flat_ids * capacity + slot_rank
    source = jnp.arange(token_count * top_count, dtype=jnp.int32) // top_count
    packed = (
        jnp.zeros((experts * capacity, features), jnp.bfloat16).at[slot_index].set(tokens[source])
    )
    received = lax.all_to_all(
        packed.reshape(experts, capacity, features),
        ("node", "local"),
        split_axis=0,
        concat_axis=0,
        tiled=True,
    )
    in_shape = received.shape
    flat_in = received.reshape(-1, in_shape[-1])
    gate_part = jnp.dot(flat_in, w_gate[0], preferred_element_type=jnp.float32)
    up_part = jnp.dot(flat_in, w_up[0], preferred_element_type=jnp.float32)
    hidden = (jax.nn.silu(gate_part) * up_part).astype(jnp.bfloat16)
    output = jnp.dot(hidden, w_down[0], preferred_element_type=jnp.float32).astype(jnp.bfloat16)
    returned_rows = lax.all_to_all(
        output.reshape(in_shape), ("node", "local"), split_axis=0, concat_axis=0, tiled=True
    )
    returned_rows = returned_rows.reshape(experts * capacity, features)
    picked = returned_rows[slot_index].astype(jnp.float32)
    weighted = picked.reshape(token_count, top_count, features) * gate_scores[:, :, None]
    return jnp.sum(weighted, axis=1).astype(jnp.bfloat16)


def solution(mesh):
    in_specs = (
        P(("node", "local"), None),
        P(("node", "local"), None),
        P(("node", "local"), None),
        P(("node", "local"), None, None),
        P(("node", "local"), None, None),
        P(("node", "local"), None, None),
    )
    out_specs = P(("node", "local"), None)
    return jax.shard_map(
        per_device, mesh=mesh, in_specs=in_specs, out_specs=out_specs, check_vma=False
    )
```

profile of v0, /device:TPU:32, one launch (start us, length us, event | category | flops | bytes accessed | tf_op | source)
XLA Modules:
  0.0 608.6 jit_solution(8217053528703033960)
XLA Ops:
  0.0 0.9 copy.9
  0.9 0.1 eq.29
  1.1 0.7 broadcast_multiply_fusion
  1.8 0.1 copy.11
  1.9 0.2 fusion.16
  2.2 0.1 copy.12
  2.3 0.1 copy.8
  2.4 0.1 mul.36
  2.5 0.4 fusion.15
  2.9 7.7 %gather_fusion = bf16[1024,4096]{1,0:T(8,128)(2,1)} fusion(bf16[128,4096]{1,0:T(8,128)(2,1)S(1)} %copy-done, s32[1024]{0:T(1024)S(1)} %broadcast_clamp_fusion.1), kind=kCustom, calls=%fused_computation | custom fusion | bytes 16781312 | tf_op jit(solution)/shard_map/gather | solution.py:22
  10.6 18.8 %scatter_custom_fusion = bf16[1280,4096]{1,0:T(8,128)(2,1)} fusion(s32[1024]{0:T(1024)S(1)} %bitcast.33, bf16[1024,4096]{1,0:T(8,128)(2,1)} %gather_fusion, bf16[]{:T(256)} %constant.26.clone.1), kind=kCustom, calls=%fused_computation.11 | custom fusion | bytes 10486272 | tf_op jit(solution)/shard_map/scatter | solution.py:22
  29.4 15.2 %reshape.107 = bf16[128,10,4096]{2,1,0:T(8,128)(2,1)} reshape(bf16[1280,4096]{1,0:T(8,128)(2,1)} %scatter_custom_fusion) | data formatting | bytes 20971520 | tf_op jit(solution)/shard_map/reshape | solution.py:25
  44.6 198.1 %all_to_all.10 = bf16[128,10,4096]{2,1,0:T(8,128)(2,1)} all-to-all(bf16[128,10,4096]{2,1,0:T(8,128)(2,1)} %reshape.107), channel_id=1, replica_groups=mesh['node'=32,'local'=4] {'node','local'}, dimensions={0} | all-to-all | bytes 20971520 | tf_op jit(solution)/shard_map/all_to_all | solution.py:24
  242.7 16.5 %reshape.108 = bf16[1280,4096]{1,0:T(8,128)(2,1)} reshape(bf16[128,10,4096]{2,1,0:T(8,128)(2,1)} %all_to_all.10) | data formatting | bytes 20971520 | tf_op jit(solution)/shard_map/reshape | solution.py:32
  259.2 12.3 %fusion.4 = f32[1280,768]{1,0:T(8,128)S(1)} fusion(bf16[1280,4096]{1,0:T(8,128)(2,1)} %reshape.108, bf16[1,4096,768]{2,1,0:T(8,128)(2,1)} %param.9), kind=kOutput, calls=%fused_computation.9 | convolution fusion | flops 8053063680 | bytes 20709376 | tf_op jit(solution)/shard_map/dot_general | solution.py:33
  271.5 11.2 %fusion.11 = bf16[1280,768]{1,0:T(8,128)(2,1)S(1)} fusion(bf16[1280,4096]{1,0:T(8,128)(2,1)S(1)} %copy-done.2, bf16[1,4096,768]{2,1,0:T(8,128)(2,1)} %param.10, f32[1280,768]{1,0:T(8,128)S(1)} %fusion.4), kind=kOutput, calls=%fused_computation.14 | convolution fusion | flops 8058961920 | bytes 22675456 | tf_op jit(solution)/shard_map/dot_general | solution.py:34
  282.7 13.5 %convolution_convert_fusion = bf16[1280,4096]{1,0:T(8,128)(2,1)} fusion(bf16[1280,768]{1,0:T(8,128)(2,1)S(1)} %fusion.11, bf16[1,768,4096]{2,1,0:T(8,128)(2,1)} %param.11), kind=kOutput, calls=%fused_computation.5 | convolution fusion | flops 8058306560 | bytes 18743296 | tf_op jit(solution)/shard_map/dot_general | solution.py:36
  296.2 15.2 %reshape.109 = bf16[128,10,4096]{2,1,0:T(8,128)(2,1)} reshape(bf16[1280,4096]{1,0:T(8,128)(2,1)} %convolution_convert_fusion) | data formatting | bytes 20971520 | tf_op jit(solution)/shard_map/reshape | solution.py:38
  311.4 6.3 %all-to-all-start.1 = ((bf16[128,10,4096]{2,1,0:T(8,128)(2,1)}), bf16[128,10,4096]{2,1,0:T(8,128)(2,1)}, u32[]{:S(2)}, u32[]{:S(2)}) async-start(bf16[128,10,4096]{2,1,0:T(8,128)(2,1)} %reshape.109), calls=%async_computation.1 | async-start | bytes 33554432 | tf_op jit(solution)/shard_map/all_to_all | solution.py:37
  317.8 0.1 copy.13
  317.9 240.8 %all-to-all-done.1 = bf16[128,10,4096]{2,1,0:T(8,128)(2,1)} async-done(((bf16[128,10,4096]{2,1,0:T(8,128)(2,1)}), bf16[128,10,4096]{2,1,0:T(8,128)(2,1)}, u32[]{:S(2)}, u32[]{:S(2)}) %all-to-all-start.1) | async-done | bytes 10485792 | tf_op jit(solution)/shard_map/all_to_all | solution.py:37
  558.7 16.5 %reshape.110 = bf16[1280,4096]{1,0:T(8,128)(2,1)} reshape(bf16[128,10,4096]{2,1,0:T(8,128)(2,1)} %all-to-all-done.1) | data formatting | bytes 20971520 | tf_op jit(solution)/shard_map/reshape | solution.py:40
  575.2 20.5 %gather_fusion.1 = bf16[1024,4096]{1,0:T(8,128)(2,1)} fusion(bf16[1280,4096]{1,0:T(8,128)(2,1)} %reshape.110, s32[1024]{0:T(1024)S(1)} %broadcast_clamp_fusion), kind=kCustom, calls=%fused_computation.1 | custom fusion | bytes 16781312 | tf_op jit(solution)/shard_map/gather | solution.py:41
  595.7 12.9 %fusion = bf16[128,4096]{1,0:T(8,128)(2,1)} fusion(bf16[1024,4096]{1,0:T(8,128)(2,1)} %gather_fusion.1, f32[128,8]{1,0:T(8,128)S(1)} %copy.13), kind=kLoop, calls=%fused_computation.4 | loop fusion | flops 12058624 | bytes 9441280 | tf_op jit(solution)/shard_map/reduce_sum | solution.py:43
  (17 shorter events, 0.2 us)
Async XLA Ops:
  0.0 2.9 copy-start
  259.2 12.3 %copy-start.2 = (bf16[1280,4096]{1,0:T(8,128)(2,1)S(1)}, bf16[1280,4096]{1,0:T(8,128)(2,1)}, u32[]{:S(2)}) copy-start(bf16[1280,4096]{1,0:T(8,128)(2,1)} %reshape.108) | copy-start | bytes 31457284
  311.4 6.3 %copy-start.3 = (f32[128,8]{0,1:T(8,128)S(1)}, f32[128,8]{0,1:T(8,128)}, u32[]{:S(2)}) copy-start(f32[128,8]{0,1:T(8,128)} %param.8) | copy-start | bytes 12292
  311.4 247.2 %all-to-all-start.1 = ((bf16[128,10,4096]{2,1,0:T(8,128)(2,1)}), bf16[128,10,4096]{2,1,0:T(8,128)(2,1)}, u32[]{:S(2)}, u32[]{:S(2)}) async-start(bf16[128,10,4096]{2,1,0:T(8,128)(2,1)} %reshape.109), calls=%async_computation.1 | async-start | bytes 33554432 | tf_op jit(solution)/shard_map/all_to_all | solution.py:37
  575.2 33.4 %copy-start.1 = (bf16[128,4096]{1,0:T(8,128)(2,1)S(1)}, bf16[128,4096]{1,0:T(8,128)(2,1)}, u32[]{:S(2)}) copy-start(bf16[128,4096]{1,0:T(8,128)(2,1)} %param.6) | copy-start | bytes 3145732
where the time goes:
time: 610 us; the launch traced here: 609 us
  waiting for transfers between devices  241 us (40%)
  blocking collectives  198 us (32%)
  local copies, waits for them, and re-layouts  112 us (18%)
  matrix products  37 us (6%)
  other arithmetic  14.2 us (2%)
  starting transfers between devices  6.32 us (1%)
    all_to_all x1, waiting for transfers between devices, per_device(): lax.all_to_all(output.reshape(in_shape), ('node', 'local'), split_axis=0,...  241 us
    all_to_all x1, blocking collectives, per_device(): lax.all_to_all(packed.reshape(experts, capacity, features), ('node', 'loc...  198 us
    gather x1, local copies, waits for them, and re-layouts, per_device(): picked = returned_rows[slot_index].astype(jnp.float32)  20.5 us
    scatter x1, local copies, waits for them, and re-layouts, per_device(): jnp.zeros((experts * capacity, features), jnp.bfloat16).at[slot_index]  18.8 us
    reshape x1, local copies, waits for them, and re-layouts, per_device(): flat_in = received.reshape(-1, in_shape[-1])  16.5 us
    reshape x1, local copies, waits for them, and re-layouts, per_device(): returned_rows = returned_rows.reshape(experts * capacity, features)  16.5 us
    reshape x1, local copies, waits for them, and re-layouts, per_device(): packed.reshape(experts, capacity, features)  15.2 us
    reshape x1, local copies, waits for them, and re-layouts, per_device(): output.reshape(in_shape)  15.2 us
  transfers between devices with their start and end apart: 1, of which 1 were waited for; matrix products, arithmetic and copies ran while one was open for 0% of the time, Pallas kernels for 0%

commit v1 on v0

v1 whole, which is shorter than its diff:
```python
import jax
import jax.numpy as jnp
from jax import lax
from jax.sharding import PartitionSpec as P

MAIN = 8
FOLD = 4


def per_device(tokens, expert_ids, gate_scores, w_gate, w_up, w_down):
    axes = ("node", "local")
    experts = lax.axis_size("node") * lax.axis_size("local")
    token_count, features = tokens.shape
    quarter = features // FOLD
    f32, bf16 = jnp.float32, jnp.bfloat16

    expert_range = jnp.arange(experts, dtype=jnp.int32)
    match = expert_ids[:, :, None] == expert_range[None, None, :]
    chosen = jnp.any(match, axis=1)
    weight = jnp.sum(jnp.where(match, gate_scores[:, :, None], 0.0), axis=1)
    row = lax.broadcasted_iota(jnp.int32, (token_count, token_count), 0)
    col = lax.broadcasted_iota(jnp.int32, (token_count, token_count), 1)
    rank = jnp.dot((col < row).astype(bf16), chosen.astype(bf16), preferred_element_type=f32)
    rank = jnp.where(chosen, rank.astype(jnp.int32), -1)
    rank_t = rank.T

    sub = jnp.arange(MAIN, dtype=jnp.int32)
    pick_main = (rank_t[:, None, :] == sub[None, :, None]).astype(bf16)
    pick_main = pick_main.reshape(experts * MAIN, token_count)
    fold_hit = rank_t[:, None, :] == (MAIN + sub // FOLD)[None, :, None]
    fold_of = sub % FOLD
    main = jnp.dot(pick_main, tokens, preferred_element_type=f32).astype(bf16)
    extra = jnp.zeros((experts * MAIN, quarter), f32)
    for part in range(FOLD):
        pick = (fold_hit & (fold_of == part)[None, :, None]).astype(bf16)
        extra = extra + jnp.dot(
            pick.reshape(experts * MAIN, token_count),
            tokens[:, part * quarter : (part + 1) * quarter],
            preferred_element_type=f32,
        )
    extra = extra.astype(bf16)

    def exchange(block, width):
        block = block.reshape(experts, MAIN, width)
        return lax.all_to_all(block, axes, split_axis=0, concat_axis=0, tiled=True).reshape(
            experts * MAIN, width
        )

    main = exchange(main, features)
    extra = exchange(extra, quarter)

    over = MAIN // FOLD * experts
    over_row = lax.broadcasted_iota(jnp.int32, (over, experts * MAIN), 0)
    sub_row = lax.broadcasted_iota(jnp.int32, (over, experts * MAIN), 1)
    folds = [(sub_row == FOLD * over_row + part).astype(bf16) for part in range(FOLD)]
    extra_rows = jnp.concatenate(
        [jnp.dot(f, extra, preferred_element_type=f32).astype(bf16) for f in folds], axis=1
    )

    def expert(rows):
        gate_part = jnp.dot(rows, w_gate[0], preferred_element_type=f32)
        up_part = jnp.dot(rows, w_up[0], preferred_element_type=f32)
        hidden = (jax.nn.silu(gate_part) * up_part).astype(bf16)
        return jnp.dot(hidden, w_down[0], preferred_element_type=f32).astype(bf16)

    main = expert(main)
    extra_rows = expert(extra_rows)
    extra = jnp.zeros((experts * MAIN, quarter), f32)
    for part in range(FOLD):
        extra = extra + jnp.dot(
            folds[part].T,
            extra_rows[:, part * quarter : (part + 1) * quarter],
            preferred_element_type=f32,
        )
    extra = extra.astype(bf16)

    main = exchange(main, features)
    extra = exchange(extra, quarter)

    high = lax.reduce_precision(weight, 8, 7)
    parts = jnp.concatenate([high, weight - high], axis=0).astype(bf16)
    rank2 = jnp.concatenate([rank, rank], axis=0)
    put_main = jnp.where(rank2[:, :, None] == sub[None, None, :], parts[:, :, None], 0)
    put_main = put_main.reshape(2 * token_count, experts * MAIN).astype(bf16)
    put_hit = rank2[:, :, None] == (MAIN + sub // FOLD)[None, None, :]
    total = jnp.dot(put_main, main, preferred_element_type=f32)
    cols = []
    for part in range(FOLD):
        put = jnp.where(put_hit & (fold_of == part)[None, None, :], parts[:, :, None], 0)
        put = put.reshape(2 * token_count, experts * MAIN).astype(bf16)
        cols.append(jnp.dot(put, extra, preferred_element_type=f32))
    total = total + jnp.concatenate(cols, axis=1)
    return (total[:token_count] + total[token_count:]).astype(bf16)


def solution(mesh):
    in_specs = (
        P(("node", "local"), None),
        P(("node", "local"), None),
        P(("node", "local"), None),
        P(("node", "local"), None, None),
        P(("node", "local"), None, None),
        P(("node", "local"), None, None),
    )
    out_specs = P(("node", "local"), None)
    return jax.shard_map(
        per_device, mesh=mesh, in_specs=in_specs, out_specs=out_specs, check_vma=False
    )
```

time: 610 us -> 330 us (0.54)
  the two profiles are of different devices: /device:TPU:32 before, /device:TPU:1 now
where the time goes in v1:
time: 330 us; the launch traced here: 324 us
  waiting for transfers between devices  193 us (58%)
  matrix products  92.8 us (28%)
  starting transfers between devices  33.3 us (10%)
    all_to_all x4, waiting for transfers between devices, exchange(): lax.all_to_all(block, axes, split_axis=0, concat_axis=0, tiled=True)  193 us
    all_to_all x4, starting transfers between devices, exchange(): lax.all_to_all(block, axes, split_axis=0, concat_axis=0, tiled=True)  33.3 us
    dot_general x2, matrix products, expert(): return jnp.dot(hidden, w_down[0], preferred_element_type=f32).astype(bf16)  18.6 us
    dot_general x2, matrix products, expert(): gate_part = jnp.dot(rows, w_gate[0], preferred_element_type=f32)  16 us
    dot_general x1, matrix products, per_device(): total = jnp.dot(put_main, main, preferred_element_type=f32)  14.6 us
    dot_general x4, matrix products, per_device(): cols.append(jnp.dot(put, extra, preferred_element_type=f32))  13.5 us
    dot_general x1, matrix products, expert(): up_part = jnp.dot(rows, w_up[0], preferred_element_type=f32)  11 us
  transfers between devices with their start and end apart: 4, of which 3 were waited for; matrix products, arithmetic and copies ran while one was open for 23% of the time, Pallas kernels for 0%

profile of v1, /device:TPU:1, one launch (start us, length us, event | category | flops | bytes accessed | tf_op | source)
XLA Modules:
  0.0 324.4 jit_solution(953671064547891430)
XLA Ops:
  1.9 1.7 fusion.111
  5.2 2.3 fusion.37
  7.5 11.5 %all-to-all-start.2 = ((bf16[128,8,1024]{2,1,0:T(8,128)(2,1)}), bf16[128,8,1024]{2,1,0:T(8,128)(2,1)S(1)}, u32[]{:S(2)}, u32[]{:S(2)}) async-start(bf16[128,8,1024]{2,1,0:T(8,128)(2,1)} %fusion.37), calls=%async_computation.2 | async-start | bytes 4194304 | tf_op jit(solution)/shard_map/all_to_all | solution.py:45
  19.1 5.6 %convert_bitcast_fusion.1 = bf16[128,8,4096]{2,1,0:T(8,128)(2,1)} fusion(bf16[128,4096]{1,0:T(8,128)(2,1)S(1)} %copy-done, s32[1024]{0:T(1024)S(1)} %eq.163, s32[128,128]{1,0:T(8,128)S(1)} %copy.27), kind=kOutput, calls=%fused_computation.7 | convolution fusion | flops 1078067200 | bytes 9506816 | tf_op jit(solution)/shard_map/dot_general | solution.py:32
  24.7 25.0 %all-to-all-done.2 = bf16[128,8,1024]{2,1,0:T(8,128)(2,1)S(1)} async-done(((bf16[128,8,1024]{2,1,0:T(8,128)(2,1)}), bf16[128,8,1024]{2,1,0:T(8,128)(2,1)S(1)}, u32[]{:S(2)}, u32[]{:S(2)}) %all-to-all-start.2) | async-done | bytes 2097184 | tf_op jit(solution)/shard_map/all_to_all | solution.py:45
  49.8 5.5 %all-to-all-start = ((bf16[128,8,4096]{2,1,0:T(8,128)(2,1)}), bf16[128,8,4096]{2,1,0:T(8,128)(2,1)}, u32[]{:S(2)}, u32[]{:S(2)}) async-start(bf16[128,8,4096]{2,1,0:T(8,128)(2,1)} %convert_bitcast_fusion.1), calls=%async_computation | async-start | bytes 16777216 | tf_op jit(solution)/shard_map/all_to_all | solution.py:45
  59.3 4.6 %fusion.12 = f32[256,768]{1,0:T(8,128)S(1)} fusion(bf16[1,4096,768]{2,1,0:T(8,128)(2,1)} %param.9, bf16[256,1024]{1,0:T(8,128)(2,1)S(1)} %fusion.52, bf16[256,1024]{1,0:T(8,128)(2,1)S(1)} %fusion.49, bf16[256,1024]{1,0:T(8,128)(2,1)S(1)} %fusion.46, bf16[256,1024]{1,0:T(8,128)(2,1)S(1)} %fusion.43), kind=kOutput, calls=%fused_computation.14 | convolution fusion | flops 1619001344 | bytes 9175040 | tf_op jit(solution)/shard_map/dot_general | solution.py:61
  63.9 9.8 %fusion.21 = bf16[256,4096]{1,0:T(8,128)(2,1)S(1)} fusion(bf16[1,768,4096]{2,1,0:T(8,128)(2,1)} %param.11, bf16[1,4096,768]{2,1,0:T(8,128)(2,1)} %param.10, f32[256,768]{1,0:T(8,128)S(1)} %fusion.12, bf16[256,1024]{1,0:T(8,128)(2,1)} %copy-done.4, bf16[256,1024]{1,0:T(8,128)(2,1)} %copy-done.3, bf16[256,1024]{1,0:T(8,128)(2,1)} %copy-done.2, ...), kind=kOutput, calls=%fused_computation.19 | convolution fusion | flops 3231842304 | bytes 17563648 | tf_op jit(solution)/shard_map/dot_general | solution.py:64
  73.7 0.8 fusion.62
  75.3 0.8 fusion.64
  76.2 2.3 fusion.38
  78.4 79.3 %all-to-all-done = bf16[128,8,4096]{2,1,0:T(8,128)(2,1)} async-done(((bf16[128,8,4096]{2,1,0:T(8,128)(2,1)}), bf16[128,8,4096]{2,1,0:T(8,128)(2,1)}, u32[]{:S(2)}, u32[]{:S(2)}) %all-to-all-start) | async-done | bytes 8388640 | tf_op jit(solution)/shard_map/all_to_all | solution.py:45
  157.7 6.0 %all-to-all-start.3 = ((bf16[128,8,1024]{2,1,0:T(8,128)(2,1)}), bf16[128,8,1024]{2,1,0:T(8,128)(2,1)S(1)}, u32[]{:S(2)}, u32[]{:S(2)}) async-start(bf16[128,8,1024]{2,1,0:T(8,128)(2,1)} %fusion.38), calls=%async_computation.3 | async-start | bytes 4194304 | tf_op jit(solution)/shard_map/all_to_all | solution.py:45
  163.7 11.0 %fusion = f32[1024,768]{1,0:T(8,128)S(1)} fusion(bf16[128,8,4096]{2,1,0:T(8,128)(2,1)} %all-to-all-done, bf16[1,4096,768]{2,1,0:T(8,128)(2,1)} %param.10), kind=kOutput, calls=%fused_computation | convolution fusion | flops 6442450944 | bytes 17825792 | tf_op jit(solution)/shard_map/dot_general | solution.py:62
  174.8 11.4 %multiply_convert_fusion = bf16[1024,768]{1,0:T(8,128)(2,1)S(1)} fusion(f32[1024,768]{1,0:T(8,128)S(1)} %fusion, bf16[1,4096,768]{2,1,0:T(8,128)(2,1)} %param.9, bf16[128,8,4096]{2,1,0:T(8,128)(2,1)} %all-to-all-done), kind=kOutput, calls=%fused_computation.22 | convolution fusion | flops 6447169536 | bytes 19398656 | tf_op jit(solution)/shard_map/dot_general | solution.py:61
  186.2 8.9 %convert_bitcast_fusion = bf16[128,8,4096]{2,1,0:T(8,128)(2,1)} fusion(bf16[1024,768]{1,0:T(8,128)(2,1)S(1)} %multiply_convert_fusion, bf16[1,768,4096]{2,1,0:T(8,128)(2,1)S(1)} %bitcast.91), kind=kOutput, calls=%fused_computation.6 | convolution fusion | flops 6446645248 | bytes 16252928 | tf_op jit(solution)/shard_map/dot_general | solution.py:64
  195.0 10.4 %all-to-all-start.1 = ((bf16[128,8,4096]{2,1,0:T(8,128)(2,1)}), bf16[128,8,4096]{2,1,0:T(8,128)(2,1)}, u32[]{:S(2)}, u32[]{:S(2)}) async-start(bf16[128,8,4096]{2,1,0:T(8,128)(2,1)} %convert_bitcast_fusion), calls=%async_computation.1 | async-start | bytes 16777216 | tf_op jit(solution)/shard_map/all_to_all | solution.py:45
  205.9 2.6 convolution_bitcast_fusion.2
  208.6 3.6 %convolution_bitcast_fusion.1 = f32[256,1024]{1,0:T(8,128)} fusion(bf16[128,8,1024]{2,1,0:T(8,128)(2,1)S(1)} %all-to-all-done.3, s32[256,128]{1,0:T(8,128)S(1)} %pad_add_fusion, s32[8]{0:T(128)S(1)} %fusion.147, pred[8]{0:T(512)(128)(4,1)S(1)} %broadcast_compare_fusion, bf16[256,128]{1,0:T(8,128)(2,1)S(1)} %pad_maximum_fusion.4), kind=kOutput, calls=%fused_computation.41 | convolution fusion | flops 537657344 | bytes 3342376 | tf_op jit(solution)/shard_map/dot_general | solution.py:91
  212.2 3.6 %convolution_bitcast_fusion = f32[256,1024]{1,0:T(8,128)} fusion(bf16[128,8,1024]{2,1,0:T(8,128)(2,1)S(1)} %all-to-all-done.3, s32[256,128]{1,0:T(8,128)S(1)} %pad_add_fusion, s32[8]{0:T(128)S(1)} %fusion.147, pred[8]{0:T(512)(128)(4,1)S(1)} %broadcast_compare_fusion.2, bf16[256,128]{1,0:T(8,128)(2,1)S(1)} %pad_maximum_fusion.4), kind=kOutput, calls=%fused_computation.40 | convolution fusion | flops 537657344 | bytes 3342376 | tf_op jit(solution)/shard_map/dot_general | solution.py:91
  215.8 3.6 %convolution_bitcast_fusion.3 = f32[256,1024]{1,0:T(8,128)} fusion(bf16[128,8,1024]{2,1,0:T(8,128)(2,1)S(1)} %all-to-all-done.3, s32[256,128]{1,0:T(8,128)S(1)} %pad_add_fusion, s32[8]{0:T(128)S(1)} %fusion.147, pred[8]{0:T(512)(128)(4,1)S(1)} %broadcast_compare_fusion.1, bf16[256,128]{1,0:T(8,128)(2,1)S(1)} %pad_maximum_fusion.4), kind=kOutput, calls=%fused_computation.43 | convolution fusion | flops 537657344 | bytes 3342376 | tf_op jit(solution)/shard_map/dot_general | solution.py:91
  219.4 89.0 %all-to-all-done.1 = bf16[128,8,4096]{2,1,0:T(8,128)(2,1)} async-done(((bf16[128,8,4096]{2,1,0:T(8,128)(2,1)}), bf16[128,8,4096]{2,1,0:T(8,128)(2,1)}, u32[]{:S(2)}, u32[]{:S(2)}) %all-to-all-start.1) | async-done | bytes 8388640 | tf_op jit(solution)/shard_map/all_to_all | solution.py:45
  308.4 14.6 %fusion.18 = f32[256,4096]{1,0:T(8,128)S(1)} fusion(bf16[128,8,4096]{2,1,0:T(8,128)(2,1)} %all-to-all-done.1, f32[256,1024]{1,0:T(8,128)} %convolution_bitcast_fusion, f32[256,1024]{1,0:T(8,128)} %convolution_bitcast_fusion.1, f32[256,1024]{1,0:T(8,128)S(1)} %convolution_bitcast_fusion.2, f32[256,1024]{1,0:T(8,128)} %convolution_bitcast_fusion.3, ...), kind=kOutput, calls=%fused_computation.18 | convolution fusion | flops 2152202240 | bytes 16973824 | tf_op jit(solution)/shard_map/dot_general | solution.py:86
  323.0 1.2 fusion.28
  (55 shorter events, 8.7 us)
Async XLA Ops:
  0.0 3.6 %copy-start = (bf16[128,4096]{1,0:T(8,128)(2,1)S(1)}, bf16[128,4096]{1,0:T(8,128)(2,1)}, u32[]{:S(2)}) copy-start(bf16[128,4096]{1,0:T(8,128)(2,1)} %param.6) | copy-start | bytes 3145732
  7.5 42.3 %all-to-all-start.2 = ((bf16[128,8,1024]{2,1,0:T(8,128)(2,1)}), bf16[128,8,1024]{2,1,0:T(8,128)(2,1)S(1)}, u32[]{:S(2)}, u32[]{:S(2)}) async-start(bf16[128,8,1024]{2,1,0:T(8,128)(2,1)} %fusion.37), calls=%async_computation.2 | async-start | bytes 4194304 | tf_op jit(solution)/shard_map/all_to_all | solution.py:45
  49.8 108.0 %all-to-all-start = ((bf16[128,8,4096]{2,1,0:T(8,128)(2,1)}), bf16[128,8,4096]{2,1,0:T(8,128)(2,1)}, u32[]{:S(2)}, u32[]{:S(2)}) async-start(bf16[128,8,4096]{2,1,0:T(8,128)(2,1)} %convert_bitcast_fusion.1), calls=%async_computation | async-start | bytes 16777216 | tf_op jit(solution)/shard_map/all_to_all | solution.py:45
  56.1 2.4 copy-start.2
  56.8 1.6 copy-start.3
  57.6 0.8 copy-start.4
  58.5 0.8 copy-start.5
  157.7 37.3 %all-to-all-start.3 = ((bf16[128,8,1024]{2,1,0:T(8,128)(2,1)}), bf16[128,8,1024]{2,1,0:T(8,128)(2,1)S(1)}, u32[]{:S(2)}, u32[]{:S(2)}) async-start(bf16[128,8,1024]{2,1,0:T(8,128)(2,1)} %fusion.38), calls=%async_computation.3 | async-start | bytes 4194304 | tf_op jit(solution)/shard_map/all_to_all | solution.py:45
  163.7 22.5 %slice-start = ((s8[6291456]{0:T(1024)(128)(4,1)}), s8[4194304]{0:T(1024)(128)(4,1)S(1)}, s32[]{:S(2)}) async-start(s8[6291456]{0:T(1024)(128)(4,1)} %bitcast.90), calls=%async_computation.4 | async-start | bytes 8388608
  174.7 11.4 %slice-start.1 = ((s8[6291456]{0:T(1024)(128)(4,1)}), s8[2097152]{0:T(1024)(128)(4,1)S(1)}, s32[]{:S(2)}) async-start(s8[6291456]{0:T(1024)(128)(4,1)} %bitcast.90), calls=%async_computation.5 | async-start | bytes 4194304
  195.0 10.4 %copy-start.1 = (f32[128,8]{0,1:T(8,128)S(1)}, f32[128,8]{0,1:T(8,128)}, u32[]{:S(2)}) copy-start(f32[128,8]{0,1:T(8,128)} %param.8) | copy-start | bytes 12292
  195.0 113.3 %all-to-all-start.1 = ((bf16[128,8,4096]{2,1,0:T(8,128)(2,1)}), bf16[128,8,4096]{2,1,0:T(8,128)(2,1)}, u32[]{:S(2)}, u32[]{:S(2)}) async-start(bf16[128,8,4096]{2,1,0:T(8,128)(2,1)} %convert_bitcast_fusion), calls=%async_computation.1 | async-start | bytes 16777216 | tf_op jit(solution)/shard_map/all_to_all | solution.py:45

commit v2 on v1

v2 whole, which is shorter than its diff:
```python
import jax
import jax.numpy as jnp
from jax import lax
from jax.sharding import PartitionSpec as P

MAIN = 8
FOLD = 4


def per_device(tokens, expert_ids, gate_scores, w_gate, w_up, w_down):
    axes = ("node", "local")
    experts = lax.axis_size("node") * lax.axis_size("local")
    token_count, features = tokens.shape
    quarter = features // FOLD
    slots = experts * MAIN
    f32, bf16 = jnp.float32, jnp.bfloat16

    expert_range = jnp.arange(experts, dtype=jnp.int32)
    match = expert_ids[:, :, None] == expert_range[None, None, :]
    chosen = jnp.any(match, axis=1)
    row = lax.broadcasted_iota(jnp.int32, (token_count, token_count), 0)
    col = lax.broadcasted_iota(jnp.int32, (token_count, token_count), 1)
    rank = jnp.dot((col < row).astype(bf16), chosen.astype(bf16), preferred_element_type=f32)
    rank = jnp.where(chosen, rank.astype(jnp.int32), -1)
    rank_t = rank.T

    sub = jnp.arange(MAIN, dtype=jnp.int32)
    fold_of = sub % FOLD
    part_range = jnp.arange(FOLD, dtype=jnp.int32)

    def exchange(block, width):
        block = block.reshape(experts, MAIN, width)
        return lax.all_to_all(block, axes, split_axis=0, concat_axis=0, tiled=True).reshape(
            slots, width
        )

    pick_main = (rank_t[:, None, :] == sub[None, :, None]).astype(bf16)
    main = jnp.dot(
        pick_main.reshape(slots, token_count), tokens, preferred_element_type=f32
    ).astype(bf16)
    main = exchange(main, features)

    fold_hit = rank_t[:, None, :] == (MAIN + sub // FOLD)[None, :, None]
    extra = jnp.zeros((slots, quarter), f32)
    for part in range(FOLD):
        pick = (fold_hit & (fold_of == part)[None, :, None]).astype(bf16)
        extra = extra + jnp.dot(
            pick.reshape(slots, token_count),
            tokens[:, part * quarter : (part + 1) * quarter],
            preferred_element_type=f32,
        )
    extra = extra.astype(bf16)
    extra, main = lax.optimization_barrier((extra, main))
    extra = exchange(extra, quarter)

    def expert(rows):
        gate_part = jnp.dot(rows, w_gate[0], preferred_element_type=f32)
        up_part = jnp.dot(rows, w_up[0], preferred_element_type=f32)
        hidden = (jax.nn.silu(gate_part) * up_part).astype(bf16)
        return jnp.dot(hidden, w_down[0], preferred_element_type=f32).astype(bf16)

    main = expert(main)
    main, extra = lax.optimization_barrier((main, extra))
    main_back = exchange(main, features)

    over = MAIN // FOLD * experts
    over_row = lax.broadcasted_iota(jnp.int32, (over, slots), 0)
    sub_row = lax.broadcasted_iota(jnp.int32, (over, slots), 1)
    folds = [(sub_row == FOLD * over_row + part).astype(bf16) for part in range(FOLD)]
    extra_rows = jnp.concatenate(
        [jnp.dot(f, extra, preferred_element_type=f32).astype(bf16) for f in folds], axis=1
    )
    extra_rows = expert(extra_rows)
    extra = jnp.zeros((slots, quarter), f32)
    for part in range(FOLD):
        extra = extra + jnp.dot(
            folds[part].T,
            extra_rows[:, part * quarter : (part + 1) * quarter],
            preferred_element_type=f32,
        )
    extra = extra.astype(bf16)

    weight = jnp.sum(jnp.where(match, gate_scores[:, :, None], 0.0), axis=1)
    put_main = jnp.where(rank[:, :, None] == sub[None, None, :], weight[:, :, None], 0.0)
    put_main = put_main.astype(bf16).reshape(token_count, slots)
    put_hit = rank[:, :, None] == (MAIN + sub // FOLD)[None, None, :]
    put_extra = jnp.where(
        put_hit[None] & (fold_of[None, :] == part_range[:, None])[:, None, None, :],
        weight[None, :, :, None],
        0.0,
    )
    put_extra = put_extra.astype(bf16).reshape(FOLD * token_count, slots)

    extra, main_back, put_extra, put_main = lax.optimization_barrier(
        (extra, main_back, put_extra, put_main)
    )
    extra_back = exchange(extra, quarter)

    total = jnp.dot(put_main, main_back, preferred_element_type=f32)
    total, extra_back = lax.optimization_barrier((total, extra_back))
    quarters = jnp.dot(put_extra, extra_back, preferred_element_type=f32)
    quarters = quarters.reshape(FOLD, token_count, quarter)
    total = total + jnp.concatenate([quarters[part] for part in range(FOLD)], axis=1)
    return total.astype(bf16)


def solution(mesh):
    in_specs = (
        P(("node", "local"), None),
        P(("node", "local"), None),
        P(("node", "local"), None),
        P(("node", "local"), None, None),
        P(("node", "local"), None, None),
        P(("node", "local"), None, None),
    )
    out_specs = P(("node", "local"), None)
    return jax.shard_map(
        per_device, mesh=mesh, in_specs=in_specs, out_specs=out_specs, check_vma=False
    )
```

time: 330 us -> 313 us (0.948); the launches traced: 324 us -> 312 us
  matrix products: 92.8 us -> 71.2 us
  waiting for transfers between devices: 193 us -> 202 us
    dot_general x10 -> x7, matrix products: 39.2 us -> 19 us  [the longest x1 6.85 us: per_device(): jnp.dot(pick_main.reshape(slots, token_count), tokens, preferred_element_...]
    all_to_all x4, waiting for transfers between devices: 193 us -> 202 us  [exchange(): lax.all_to_all(block, axes, split_axis=0, concat_axis=0, tiled=True)]
  transfers between devices with their start and end apart: 4 -> 4, of which waited for: 3 -> 3; matrix products, arithmetic and copies ran while one was open for 23% -> 21% of each run, Pallas kernels for 0% -> 0%
where the time goes in v2:
time: 313 us; the launch traced here: 312 us
  waiting for transfers between devices  202 us (65%)
  matrix products  71.2 us (23%)
  starting transfers between devices  31.9 us (10%)
  other arithmetic  3.18 us (1%)
    all_to_all x4, waiting for transfers between devices, exchange(): lax.all_to_all(block, axes, split_axis=0, concat_axis=0, tiled=True)  202 us
    all_to_all x4, starting transfers between devices, exchange(): lax.all_to_all(block, axes, split_axis=0, concat_axis=0, tiled=True)  31.9 us
    dot_general x2, matrix products, expert(): return jnp.dot(hidden, w_down[0], preferred_element_type=f32).astype(bf16)  18.8 us
    dot_general x2, matrix products, expert(): gate_part = jnp.dot(rows, w_gate[0], preferred_element_type=f32)  14 us
    dot_general x1, matrix products, expert(): up_part = jnp.dot(rows, w_up[0], preferred_element_type=f32)  11 us
    dot_general x1, matrix products, per_device(): jnp.dot(pick_main.reshape(slots, token_count), tokens, preferred_element_...  6.85 us
  transfers between devices with their start and end apart: 4, of which 3 were waited for; matrix products, arithmetic and copies ran while one was open for 21% of the time, Pallas kernels for 0%

profile of v2, /device:TPU:1, one launch (start us, length us, event | category | flops | bytes accessed | tf_op | source)
XLA Modules:
  0.0 312.1 jit_solution(2700009593166408500)
XLA Ops:
  0.0 0.8 copy.14
  1.4 6.9 %convert_bitcast_fusion = bf16[128,8,4096]{2,1,0:T(8,128)(2,1)} fusion(bf16[128,4096]{1,0:T(8,128)(2,1)} %param.6, s32[1024]{0:T(1024)S(1)} %eq.169, s32[128,128]{1,0:T(8,128)S(1)} %copy.15), kind=kOutput, calls=%fused_computation | convolution fusion | flops 1078067200 | bytes 9506816 | tf_op jit(solution)/shard_map/dot_general | solution.py:38
  8.3 11.9 %all-to-all-start = ((bf16[128,8,4096]{2,1,0:T(8,128)(2,1)}), bf16[128,8,4096]{2,1,0:T(8,128)(2,1)}, u32[]{:S(2)}, u32[]{:S(2)}) async-start(bf16[128,8,4096]{2,1,0:T(8,128)(2,1)} %convert_bitcast_fusion), calls=%async_computation | async-start | bytes 16777216 | tf_op jit(solution)/shard_map/all_to_all | solution.py:33
  23.1 2.3 add_convert_fusion.1
  25.5 97.8 %all-to-all-done = bf16[128,8,4096]{2,1,0:T(8,128)(2,1)} async-done(((bf16[128,8,4096]{2,1,0:T(8,128)(2,1)}), bf16[128,8,4096]{2,1,0:T(8,128)(2,1)}, u32[]{:S(2)}, u32[]{:S(2)}) %all-to-all-start) | async-done | bytes 8388640 | tf_op jit(solution)/shard_map/all_to_all | solution.py:33
  123.3 4.6 %all-to-all-start.1 = ((bf16[128,8,1024]{2,1,0:T(8,128)(2,1)}), bf16[128,8,1024]{2,1,0:T(8,128)(2,1)S(1)}, u32[]{:S(2)}, u32[]{:S(2)}) async-start(bf16[128,8,1024]{2,1,0:T(8,128)(2,1)} %bitcast.7), calls=%async_computation.1 | async-start | bytes 4194304 | tf_op jit(solution)/shard_map/all_to_all | solution.py:33
  127.9 11.0 %fusion.5 = f32[1024,768]{1,0:T(8,128)S(1)} fusion(bf16[1024,4096]{1,0:T(8,128)(2,1)} %bitcast.3, bf16[1,4096,768]{2,1,0:T(8,128)(2,1)} %param.10), kind=kOutput, calls=%fused_computation.7 | convolution fusion | flops 6442450944 | bytes 17825792 | tf_op jit(solution)/shard_map/dot_general | solution.py:58
  139.0 11.4 %multiply_convert_fusion = bf16[1024,768]{1,0:T(8,128)(2,1)S(1)} fusion(f32[1024,768]{1,0:T(8,128)S(1)} %fusion.5, bf16[1024,4096]{1,0:T(8,128)(2,1)} %bitcast.3, bf16[1,4096,768]{2,1,0:T(8,128)(2,1)} %param.9), kind=kOutput, calls=%fused_computation.16 | convolution fusion | flops 6447169536 | bytes 19398656 | tf_op jit(solution)/shard_map/dot_general | solution.py:57
  150.4 8.8 %convolution_convert_fusion = bf16[1024,4096]{1,0:T(8,128)(2,1)} fusion(bf16[1024,768]{1,0:T(8,128)(2,1)S(1)} %multiply_convert_fusion, bf16[1,768,4096]{2,1,0:T(8,128)(2,1)S(1)} %bitcast.90), kind=kOutput, calls=%fused_computation.1 | convolution fusion | flops 6446645248 | bytes 16252928 | tf_op jit(solution)/shard_map/dot_general | solution.py:60
  159.2 10.4 %all-to-all-start.2 = ((bf16[128,8,4096]{2,1,0:T(8,128)(2,1)}), bf16[128,8,4096]{2,1,0:T(8,128)(2,1)}, u32[]{:S(2)}, u32[]{:S(2)}) async-start(bf16[128,8,4096]{2,1,0:T(8,128)(2,1)} %bitcast.80), calls=%async_computation.2 | async-start | bytes 16777216 | tf_op jit(solution)/shard_map/all_to_all | solution.py:33
  170.6 0.9 fusion.24
  175.1 0.8 copy-done.5
  175.9 2.7 fusion.7
  178.6 10.0 %fusion.11 = bf16[256,4096]{1,0:T(8,128)(2,1)S(1)} fusion(bf16[1,768,4096]{2,1,0:T(8,128)(2,1)} %param.11, bf16[1,4096,768]{2,1,0:T(8,128)(2,1)} %param.10, f32[256,768]{1,0:T(8,128)} %fusion.7, bf16[256,1024]{1,0:T(8,128)(2,1)} %copy-done.2, bf16[256,1024]{1,0:T(8,128)(2,1)} %copy-done.3, bf16[256,1024]{1,0:T(8,128)(2,1)} %copy-done.4, ...), kind=kOutput, calls=%fused_computation.13 | convolution fusion | flops 3231842304 | bytes 17563648 | tf_op jit(solution)/shard_map/dot_general | solution.py:60
  188.6 0.8 fusion.26
  189.4 0.8 fusion.27
  190.2 0.8 fusion.25
  191.1 2.7 add_convert_fusion
  193.7 78.8 %all-to-all-done.2 = bf16[128,8,4096]{2,1,0:T(8,128)(2,1)} async-done(((bf16[128,8,4096]{2,1,0:T(8,128)(2,1)}), bf16[128,8,4096]{2,1,0:T(8,128)(2,1)}, u32[]{:S(2)}, u32[]{:S(2)}) %all-to-all-start.2) | async-done | bytes 8388640 | tf_op jit(solution)/shard_map/all_to_all | solution.py:33
  272.5 5.0 %all-to-all-start.3 = ((bf16[128,8,1024]{2,1,0:T(8,128)(2,1)}), bf16[128,8,1024]{2,1,0:T(8,128)(2,1)}, u32[]{:S(2)}, u32[]{:S(2)}) async-start(bf16[128,8,1024]{2,1,0:T(8,128)(2,1)} %bitcast.13), calls=%async_computation.3 | async-start | bytes 4194304 | tf_op jit(solution)/shard_map/all_to_all | solution.py:33
  277.6 4.7 %fusion.83 = f32[128,4096]{1,0:T(8,128)S(1)} fusion(bf16[128,1024]{0,1:T(8,128)(2,1)S(1)} %fusion.38, bf16[1024,4096]{1,0:T(8,128)(2,1)} %bitcast.10), kind=kOutput, calls=%fused_computation.105 | convolution fusion | flops 1073741824 | bytes 10747904 | tf_op jit(solution)/shard_map/dot_general | solution.py:99
  282.2 25.7 %all-to-all-done.3 = bf16[128,8,1024]{2,1,0:T(8,128)(2,1)} async-done(((bf16[128,8,1024]{2,1,0:T(8,128)(2,1)}), bf16[128,8,1024]{2,1,0:T(8,128)(2,1)}, u32[]{:S(2)}, u32[]{:S(2)}) %all-to-all-start.3) | async-done | bytes 2097184 | tf_op jit(solution)/shard_map/all_to_all | solution.py:33
  308.0 2.9 fusion.84
  311.0 1.2 fusion.16
  (63 shorter events, 8.0 us)
Async XLA Ops:
  8.3 12.6 %copy-start = (bf16[128,4096]{1,0:T(8,128)(2,1)S(1)}, bf16[128,4096]{1,0:T(8,128)(2,1)}, u32[]{:S(2)}) copy-start(bf16[128,4096]{1,0:T(8,128)(2,1)} %param.6) | copy-start | bytes 3145732
  8.3 115.1 %all-to-all-start = ((bf16[128,8,4096]{2,1,0:T(8,128)(2,1)}), bf16[128,8,4096]{2,1,0:T(8,128)(2,1)}, u32[]{:S(2)}, u32[]{:S(2)}) async-start(bf16[128,8,4096]{2,1,0:T(8,128)(2,1)} %convert_bitcast_fusion), calls=%async_computation | async-start | bytes 16777216 | tf_op jit(solution)/shard_map/all_to_all | solution.py:33
  123.3 35.8 %all-to-all-start.1 = ((bf16[128,8,1024]{2,1,0:T(8,128)(2,1)}), bf16[128,8,1024]{2,1,0:T(8,128)(2,1)S(1)}, u32[]{:S(2)}, u32[]{:S(2)}) async-start(bf16[128,8,1024]{2,1,0:T(8,128)(2,1)} %bitcast.7), calls=%async_computation.1 | async-start | bytes 4194304 | tf_op jit(solution)/shard_map/all_to_all | solution.py:33
  127.9 22.5 %slice-start.2 = ((s8[6291456]{0:T(1024)(128)(4,1)}), s8[4194304]{0:T(1024)(128)(4,1)S(1)}, s32[]{:S(2)}) async-start(s8[6291456]{0:T(1024)(128)(4,1)} %bitcast.89), calls=%async_computation.6 | async-start | bytes 8388608
  139.0 11.4 %slice-start.3 = ((s8[6291456]{0:T(1024)(128)(4,1)}), s8[2097152]{0:T(1024)(128)(4,1)S(1)}, s32[]{:S(2)}) async-start(s8[6291456]{0:T(1024)(128)(4,1)} %bitcast.89), calls=%async_computation.7 | async-start | bytes 4194304
  159.2 10.5 %copy-start.1 = (f32[128,8]{0,1:T(8,128)S(1)}, f32[128,8]{0,1:T(8,128)}, u32[]{:S(2)}) copy-start(f32[128,8]{0,1:T(8,128)} %param.8) | copy-start | bytes 12292
  159.2 113.3 %all-to-all-start.2 = ((bf16[128,8,4096]{2,1,0:T(8,128)(2,1)}), bf16[128,8,4096]{2,1,0:T(8,128)(2,1)}, u32[]{:S(2)}, u32[]{:S(2)}) async-start(bf16[128,8,4096]{2,1,0:T(8,128)(2,1)} %bitcast.80), calls=%async_computation.2 | async-start | bytes 16777216 | tf_op jit(solution)/shard_map/all_to_all | solution.py:33
  171.5 4.4 %slice-start = ((s8[6291456]{0:T(1024)(128)(4,1)}), s8[4194304]{0:T(1024)(128)(4,1)S(1)}, s32[]{:S(2)}) async-start(s8[6291456]{0:T(1024)(128)(4,1)} %bitcast.87), calls=%async_computation.4 | async-start | bytes 8388608
  172.7 2.3 copy-start.2
  172.7 3.2 %slice-start.1 = ((s8[6291456]{0:T(1024)(128)(4,1)}), s8[2097152]{0:T(1024)(128)(4,1)S(1)}, s32[]{:S(2)}) async-start(s8[6291456]{0:T(1024)(128)(4,1)} %bitcast.87), calls=%async_computation.5 | async-start | bytes 4194304
  173.5 1.6 copy-start.3
  174.2 0.8 copy-start.4
  175.1 0.8 copy-start.5
  272.5 35.4 %all-to-all-start.3 = ((bf16[128,8,1024]{2,1,0:T(8,128)(2,1)}), bf16[128,8,1024]{2,1,0:T(8,128)(2,1)}, u32[]{:S(2)}, u32[]{:S(2)}) async-start(bf16[128,8,1024]{2,1,0:T(8,128)(2,1)} %bitcast.13), calls=%async_computation.3 | async-start | bytes 4194304 | tf_op jit(solution)/shard_map/all_to_all | solution.py:33
